TPU v7x, 256 devices: a whole 4x4x8 slice. The times are simulated.
256 devices in a mesh: expert: 32 (over z_lo, y, core), tensor: 8 (over z_hi, x).
Axes of the slice: x: 4, y: 4, z: 8 (z_hi: 2, z_lo: 4; z = z_hi * 4 + z_lo), core: 2. Of those that a mesh axis runs over, the one named last changes fastest.
Arguments:
- tokens: bfloat16 [32768, 2048], P(('expert', 'tensor')), may hold values from -6 to 6
- assignment: int32 [32768], P(('expert', 'tensor')), may hold values from 0 to 31, as said below
- norm_gain: float32 [2048], replicated, may hold values from 0.25 to 1.75
- centroids: bfloat16 [32, 2048], replicated, may hold values from -0.125 to 0.125
- w_in: bfloat16 [32, 2048, 8192], P('expert', None, 'tensor'), may hold values from -0.125 to 0.125
- w_out: bfloat16 [32, 8192, 2048], P('expert', 'tensor'), may hold values from -0.0625 to 0.0625
Outputs:
- mixed: bfloat16 [32768, 2048], P(('expert', 'tensor'))
Inputs may be any that keep to these rules, and one draw needn't show every extreme that they name: `assignment`: in each device's block of 128 consecutive tokens every expert is named exactly 4 times.
All inputs are finite; a program needn't handle non-finite values.
Results may differ from a plain program's by a relative error of at most 0.006.
Values may be sent and summed in bfloat16 or wider, within the bound.
No kernel may reach another device: no remote copies, remote signals or barrier semaphores. Data moves between devices by JAX's collectives and lax.ppermute only.
A program may use at most 64 MiB of HBM per device.

v0:
```python
import jax
import jax.numpy as jnp
from jax import lax
from jax.sharding import Mesh
from jax.sharding import PartitionSpec as P

TENSOR = ("tensor_0", "tensor_1")
EXPERT_TENSOR = ("expert", "tensor_0", "tensor_1")


def reduced_to_own(blocks, axes, order):
    inside = blocks.shape[1:]
    blocks = blocks.reshape(*(lax.axis_size(a) for a in axes), *inside)
    blocks = jnp.moveaxis(blocks, order, range(len(axes))).reshape(-1, *inside)
    for k in order:
        blocks = lax.psum_scatter(blocks, axes[k], scatter_dimension=0, tiled=True)
    return blocks[0]


def split_up(shard, dim, size):
    lengths = shard.shape
    blocks = shard.reshape(*lengths[:dim], size, lengths[dim] // size, *lengths[dim + 1 :])
    return jnp.moveaxis(blocks, dim, 0)


def summed_rows(shard, axes, order, dim):
    size = lax.axis_size(axes)
    return reduced_to_own(split_up(shard, dim, size), axes, order)


def layer_norm(values, gain):
    widened = values.astype(jnp.float32)
    average = jnp.mean(widened, axis=1, keepdims=True)
    centred = widened - average
    variance = jnp.mean(centred * centred, axis=1, keepdims=True)
    return centred * lax.rsqrt(variance + 1e-05) * gain


def body(tokens, assignment, norm_gain, centroids, w_in, w_out):
    tok_rows = tokens.shape[0]
    num_experts = centroids.shape[0]
    per_expert = tok_rows // num_experts
    normed = layer_norm(tokens, norm_gain).astype(jnp.bfloat16)
    logits = jnp.dot(tokens, centroids.T, preferred_element_type=jnp.float32)
    column_ids = lax.broadcasted_iota(jnp.int32, (tok_rows, num_experts), 1)
    picked = jnp.sum(jnp.where(assignment[:, None] == column_ids, logits, 0.0), axis=1)
    gate_value = jax.nn.sigmoid(picked)
    same_expert = assignment[:, None] == assignment[None, :]
    row_ids = lax.broadcasted_iota(jnp.int32, (tok_rows, tok_rows), 0)
    col_ids = lax.broadcasted_iota(jnp.int32, (tok_rows, tok_rows), 1)
    rank_in = jnp.sum((same_expert & (col_ids < row_ids)).astype(jnp.int32), axis=1)
    slot_of = assignment * per_expert + rank_in
    ordering = jnp.argsort(slot_of)
    ordered_rows = normed[ordering]
    arrived = lax.all_to_all(ordered_rows, "expert", split_axis=0, concat_axis=0, tiled=True)
    w_first = w_in[0]
    w_second = w_out[0]
    hidden = jax.nn.gelu(
        jnp.dot(
            lax.all_gather(arrived, TENSOR, axis=0, tiled=True),
            w_first,
            preferred_element_type=jnp.float32,
        ),
        approximate=True,
    ).astype(jnp.bfloat16)
    partials = jnp.dot(hidden, w_second, preferred_element_type=jnp.float32).astype(jnp.bfloat16)
    summed = summed_rows(partials, TENSOR, (1, 0), 0).astype(jnp.float32).astype(jnp.bfloat16)
    returned = lax.all_to_all(summed, "expert", split_axis=0, concat_axis=0, tiled=True)
    expert_out = returned[slot_of]
    mixed = tokens.astype(jnp.float32) + gate_value[:, None] * expert_out.astype(jnp.float32)
    return mixed.astype(jnp.bfloat16)


def solution(mesh):
    finer = Mesh(
        mesh.devices.reshape(mesh.shape["expert"], 2, 4), ("expert", "tensor_0", "tensor_1")
    )
    return jax.shard_map(
        body,
        mesh=finer,
        in_specs=(
            P(EXPERT_TENSOR, None),
            P(EXPERT_TENSOR),
            P(),
            P(),
            P("expert", None, TENSOR),
            P("expert", TENSOR, None),
        ),
        out_specs=P(EXPERT_TENSOR, None),
        check_vma=False,
    )
```

profile of v0, /device:TPU:1, one launch (start us, length us, event | category | flops | bytes accessed | tf_op | source)
XLA Modules:
  0.0 288.4 jit_solution(13480588481350019458)
XLA Ops:
  6.5 0.0 copy-start
  6.5 0.0 all-gather.2.cloned.1.call-start
  6.5 1.2 convert_reduce_fusion
  7.8 1.3 fusion.23
  9.1 0.9 convert_reduce_fusion.1
  10.0 0.7 compare_select_fusion
  10.7 2.5 sort.17
  13.2 1.4 fusion.25
  14.7 0.9 gather_fusion
  15.6 0.2 all_to_all.16
  15.8 26.4 %all_to_all.24 = bf16[32,4,2048]{2,1,0:T(4,128)(2,1)S(1)} all-to-all(bf16[32,4,2048]{2,1,0:T(4,128)(2,1)S(1)} %all_to_all.16), channel_id=1, replica_groups=mesh['expert'=32,'tensor_0'=2,'tensor_1'=4] {'expert'}, dimensions={0} | all-to-all | bytes 1048576 | tf_op jit(solution)/shard_map/all_to_all | solution.py:55
  42.2 0.9 all_to_all.18
  43.1 0.0 all-gather.2.cloned.1.call-update
  43.2 0.0 reduce-scatter.3.cloned.1.call-start
  43.2 104.6 %all-gather.2.cloned.1.call-done = bf16[1024,2048]{1,0:T(8,128)(2,1)} async-done(((bf16[128,2048]{1,0:T(8,128)(2,1)}), bf16[1024,2048]{1,0:T(8,128)(2,1)}) %all-gather.2.cloned.1.call-update) | async-done | bytes 4194320 | tf_op jit(solution)/shard_map/all_gather | solution.py:60
  147.8 15.1 %fusion.12 = bf16[1024,2048]{1,0:T(8,128)(2,1)} fusion(bf16[1,1024,2048]{2,1,0:T(8,128)(2,1)} %param.11, bf16[1024,2048]{1,0:T(8,128)(2,1)} %all-gather.2.cloned.1.call-done, bf16[1,2048,1024]{2,1,0:T(8,128)(2,1)} %param.10), kind=kOutput, calls=%fused_computation.15 | convolution fusion | flops 8601468928 | bytes 16777216 | tf_op jit(solution)/shard_map/dot_general | solution.py:66
  163.0 4.7 %copy.8 = bf16[2,4,128,2048]{3,2,0,1:T(8,128)(2,1)} copy(bf16[2,4,128,2048]{3,2,1,0:T(8,128)(2,1)} %bitcast.20) | data formatting | bytes 8388608 | tf_op jit(solution)/shard_map/reshape;reshape | solution.py:13
  167.7 0.0 reduce-scatter.3.cloned.1.call-update
  167.7 0.0 reduce-scatter.5.cloned.1.call-start
  167.8 44.8 %reduce-scatter.3.cloned.1.call-done = bf16[2,128,2048]{2,1,0:T(8,128)(2,1)} async-done(((bf16[8,128,2048]{2,1,0:T(8,128)(2,1)}), bf16[2,128,2048]{2,1,0:T(8,128)(2,1)}) %reduce-scatter.3.cloned.1.call-update) | async-done | bytes 1048592 | tf_op jit(solution)/shard_map/reduce_scatter | solution.py:16
  212.5 0.0 reduce-scatter.5.cloned.1.call-update
  212.6 43.2 %reduce-scatter.5.cloned.1.call-done = bf16[1,128,2048]{2,1,0:T(8,128)(2,1)} async-done(((bf16[2,128,2048]{2,1,0:T(8,128)(2,1)}), bf16[1,128,2048]{2,1,0:T(8,128)(2,1)}) %reduce-scatter.5.cloned.1.call-update) | async-done | bytes 524304 | tf_op jit(solution)/shard_map/reduce_scatter | solution.py:16
  255.8 2.0 all_to_all.19
  257.8 5.5 %all-to-all-start.1 = ((bf16[32,4,2048]{2,1,0:T(4,128)(2,1)}), bf16[32,4,2048]{2,1,0:T(4,128)(2,1)S(1)}, u32[]{:S(2)}, u32[]{:S(2)}) async-start(bf16[32,4,2048]{2,1,0:T(4,128)(2,1)} %all_to_all.19), calls=%async_computation.3 | async-start | bytes 1048576 | tf_op jit(solution)/shard_map/all_to_all | solution.py:68
  263.3 0.0 copy-done
  263.3 0.0 copy-done.1
  263.3 0.0 copy-done.2
  263.4 0.3 fusion.22
  263.7 16.1 %all-to-all-done.1 = bf16[32,4,2048]{2,1,0:T(4,128)(2,1)S(1)} async-done(((bf16[32,4,2048]{2,1,0:T(4,128)(2,1)}), bf16[32,4,2048]{2,1,0:T(4,128)(2,1)S(1)}, u32[]{:S(2)}, u32[]{:S(2)}) %all-to-all-start.1) | async-done | bytes 524320 | tf_op jit(solution)/shard_map/all_to_all | solution.py:68
  279.7 0.1 all_to_all.21
  279.9 0.9 gather_fusion.1
  280.8 1.0 fusion.26
  (9 shorter events, 0.0 us)
Async XLA Ops:
  6.5 256.8 %copy-start = (bf16[32,2048]{1,0:T(8,128)(2,1)S(1)}, bf16[32,2048]{1,0:T(8,128)(2,1)}, u32[]{:S(2)}) copy-start(bf16[32,2048]{1,0:T(8,128)(2,1)} %param.9) | copy-start | bytes 393220
  6.5 141.3 %all-gather.2.cloned.1.call-start = ((), (), s32[]{:S(2)}) async-start(), calls=%async_computation.4 | async-start | bytes 4718592 | tf_op jit(solution)/shard_map/all_gather | solution.py:60
  43.2 169.4 %reduce-scatter.3.cloned.1.call-start = ((), (), s32[]{:S(2)}) async-start(), calls=%async_computation.5 | async-start | bytes 5242880 | tf_op jit(solution)/shard_map/reduce_scatter | solution.py:16
  167.7 95.6 %copy-start.1 = (bf16[128,2048]{1,0:T(8,128)(2,1)S(1)}, bf16[128,2048]{1,0:T(8,128)(2,1)}, u32[]{:S(2)}) copy-start(bf16[128,2048]{1,0:T(8,128)(2,1)} %param.6) | copy-start | bytes 1572868
  167.7 95.6 %copy-start.2 = (s32[128]{0:T(128)S(1)}, s32[128]{0:T(128)}, u32[]{:S(2)}) copy-start(s32[128]{0:T(128)} %param.7) | copy-start | bytes 1540
  167.7 88.1 %reduce-scatter.5.cloned.1.call-start = ((), (), s32[]{:S(2)}) async-start(), calls=%async_computation.6 | async-start | bytes 1572864 | tf_op jit(solution)/shard_map/reduce_scatter | solution.py:16
  257.8 21.9 %all-to-all-start.1 = ((bf16[32,4,2048]{2,1,0:T(4,128)(2,1)}), bf16[32,4,2048]{2,1,0:T(4,128)(2,1)S(1)}, u32[]{:S(2)}, u32[]{:S(2)}) async-start(bf16[32,4,2048]{2,1,0:T(4,128)(2,1)} %all_to_all.19), calls=%async_computation.3 | async-start | bytes 1048576 | tf_op jit(solution)/shard_map/all_to_all | solution.py:68
Sparse Core Ops, SparseCore 0:
  43.3 104.5 all-gather.1
  167.9 44.6 reduce-scatter.2
  215.0 40.6 reduce-scatter.4
where the time goes:
time: 289 us; the launch traced here: 288 us
  waiting for transfers between devices  209 us (72%)
  blocking collectives  26.4 us (9%)
  matrix products  15.4 us (5%)
  between operations  13.2 us (5%)
  local copies, waits for them, and re-layouts  9.88 us (3%)
  other arithmetic  9.13 us (3%)
  starting transfers between devices  5.57 us (2%)
    all_gather x1, waiting for transfers between devices, body(): lax.all_gather(arrived, TENSOR, axis=0, tiled=True)  105 us
    reduce_scatter x2, waiting for transfers between devices, reduced_to_own(): blocks = lax.psum_scatter(blocks, axes[k], scatter_dimension=0, tiled=True)  88 us
    all_to_all x1, blocking collectives, body(): lax.all_to_all(ordered_rows, 'expert', split_axis=0, concat_axis=0, tiled...  26.4 us
    all_to_all x1, waiting for transfers between devices, body(): lax.all_to_all(summed, 'expert', split_axis=0, concat_axis=0, tiled=True)  16.1 us
    dot_general x1, matrix products, body(): jnp.dot(hidden, w_second, preferred_element_type=jnp.float32)  15.1 us
  transfers between devices with their start and end apart: 4, of which 4 were waited for; matrix products, arithmetic and copies ran while one was open for 0% of the time, Pallas kernels for 0%

commit v1 on v0

--- a/solution.py
+++ b/solution.py
@@ -57,7 +57,9 @@
     w_second = w_out[0]
     hidden = jax.nn.gelu(
         jnp.dot(
-            lax.all_gather(arrived, TENSOR, axis=0, tiled=True),
+            jnp.concatenate(
+                lax.all_to_all(jnp.stack([arrived] * lax.axis_size(TENSOR)), TENSOR, 0, 0), axis=0
+            ),
             w_first,
             preferred_element_type=jnp.float32,
         ),

time: 289 us -> 289 us (level)
  waiting for transfers between devices: 209 us -> 115 us
  blocking collectives: 26.4 us -> 120 us
    all_gather x1 -> x0, waiting for transfers between devices: 105 us -> none  [body(): lax.all_gather(arrived, TENSOR, axis=0, tiled=True)]
    all_to_all x0 -> x1, blocking collectives: none -> 93.4 us  [body(): lax.all_to_all(jnp.stack([arrived] * lax.axis_size(TENSOR)), TENSOR, 0, 0)]
    reduce_scatter x2, waiting for transfers between devices: 88 us -> 99 us  [reduced_to_own(): blocks = lax.psum_scatter(blocks, axes[k], scatter_dimension=0, tiled=True)]
  transfers between devices with their start and end apart: 4 -> 3, of which waited for: 4 -> 3; matrix products, arithmetic and copies ran while one was open for 0% -> 0% of each run, Pallas kernels for 0% -> 0%
where the time goes in v1:
time: 289 us; the launch traced here: 288 us
  blocking collectives  120 us (42%)
  waiting for transfers between devices  115 us (40%)
  matrix products  15.4 us (5%)
  between operations  13.5 us (5%)
  local copies, waits for them, and re-layouts  9.61 us (3%)
  other arithmetic  9.13 us (3%)
  starting transfers between devices  5.49 us (2%)
    reduce_scatter x2, waiting for transfers between devices, reduced_to_own(): blocks = lax.psum_scatter(blocks, axes[k], scatter_dimension=0, tiled=True)  99 us
    all_to_all x1, blocking collectives, body(): lax.all_to_all(jnp.stack([arrived] * lax.axis_size(TENSOR)), TENSOR, 0, 0)  93.4 us
    all_to_all x1, blocking collectives, body(): lax.all_to_all(ordered_rows, 'expert', split_axis=0, concat_axis=0, tiled...  26.4 us
    all_to_all x1, waiting for transfers between devices, body(): lax.all_to_all(summed, 'expert', split_axis=0, concat_axis=0, tiled=True)  16.1 us
    dot_general x1, matrix products, body(): jnp.dot(hidden, w_second, preferred_element_type=jnp.float32)  15.1 us
  transfers between devices with their start and end apart: 3, of which 3 were waited for; matrix products, arithmetic and copies ran while one was open for 0% of the time, Pallas kernels for 0%

profile of v1, /device:TPU:1, one launch (start us, length us, event | category | flops | bytes accessed | tf_op | source)
XLA Modules:
  0.0 288.1 jit_solution(9070889836561830212)
XLA Ops:
  6.5 0.0 copy-start
  6.5 0.0 reduce-scatter.3.cloned.1.call-start
  6.5 1.2 convert_reduce_fusion
  7.8 1.3 fusion.23
  9.1 0.9 convert_reduce_fusion.1
  10.0 0.7 compare_select_fusion
  10.7 2.5 sort.17
  13.2 1.4 fusion.25
  14.7 0.9 gather_fusion
  15.6 0.2 all_to_all.17
  15.8 26.4 %all_to_all.26 = bf16[32,4,2048]{2,1,0:T(4,128)(2,1)S(1)} all-to-all(bf16[32,4,2048]{2,1,0:T(4,128)(2,1)S(1)} %all_to_all.17), channel_id=1, replica_groups=mesh['expert'=32,'tensor_0'=2,'tensor_1'=4] {'expert'}, dimensions={0} | all-to-all | bytes 1048576 | tf_op jit(solution)/shard_map/all_to_all | solution.py:55
  42.2 0.1 stack.4
  42.3 0.5 stack.5
  42.9 93.4 %all_to_all.27 = bf16[8,128,2048]{2,1,0:T(8,128)(2,1)} all-to-all(bf16[8,128,2048]{2,1,0:T(8,128)(2,1)S(1)} %stack.5), channel_id=1, replica_groups=mesh['expert'=32,'tensor_0'=2,'tensor_1'=4] {'tensor_0','tensor_1'}, dimensions={0} | all-to-all | bytes 8388608 | tf_op jit(solution)/shard_map/all_to_all | solution.py:61
  136.2 15.1 %fusion.12 = bf16[1024,2048]{1,0:T(8,128)(2,1)} fusion(bf16[1,1024,2048]{2,1,0:T(8,128)(2,1)} %param.11, bf16[1024,2048]{1,0:T(8,128)(2,1)} %bitcast.21, bf16[1,2048,1024]{2,1,0:T(8,128)(2,1)} %param.10), kind=kOutput, calls=%fused_computation.15 | convolution fusion | flops 8601468928 | bytes 16777216 | tf_op jit(solution)/shard_map/dot_general | solution.py:68
  151.4 4.7 %copy.8 = bf16[2,4,128,2048]{3,2,0,1:T(8,128)(2,1)} copy(bf16[2,4,128,2048]{3,2,1,0:T(8,128)(2,1)} %bitcast.22) | data formatting | bytes 8388608 | tf_op jit(solution)/shard_map/reshape;reshape | solution.py:13
  156.1 0.0 copy-start.1
  156.1 0.0 reduce-scatter.3.cloned.1.call-update
  156.1 0.0 reduce-scatter.5.cloned.1.call-start
  156.2 55.8 %reduce-scatter.3.cloned.1.call-done = bf16[2,128,2048]{2,1,0:T(8,128)(2,1)} async-done(((bf16[8,128,2048]{2,1,0:T(8,128)(2,1)}), bf16[2,128,2048]{2,1,0:T(8,128)(2,1)}) %reduce-scatter.3.cloned.1.call-update) | async-done | bytes 1048592 | tf_op jit(solution)/shard_map/reduce_scatter | solution.py:16
  212.0 0.0 reduce-scatter.5.cloned.1.call-update
  212.0 43.2 %reduce-scatter.5.cloned.1.call-done = bf16[1,128,2048]{2,1,0:T(8,128)(2,1)} async-done(((bf16[2,128,2048]{2,1,0:T(8,128)(2,1)}), bf16[1,128,2048]{2,1,0:T(8,128)(2,1)}) %reduce-scatter.5.cloned.1.call-update) | async-done | bytes 524304 | tf_op jit(solution)/shard_map/reduce_scatter | solution.py:16
  255.2 2.0 all_to_all.20
  257.3 5.4 %all-to-all-start.2 = ((bf16[32,4,2048]{2,1,0:T(4,128)(2,1)}), bf16[32,4,2048]{2,1,0:T(4,128)(2,1)S(1)}, u32[]{:S(2)}, u32[]{:S(2)}) async-start(bf16[32,4,2048]{2,1,0:T(4,128)(2,1)} %all_to_all.20), calls=%async_computation.4 | async-start | bytes 1048576 | tf_op jit(solution)/shard_map/all_to_all | solution.py:70
  262.7 0.0 copy-done
  262.8 0.0 copy-done.1
  262.8 0.0 copy-done.2
  262.8 0.3 fusion.22
  263.1 16.1 %all-to-all-done.2 = bf16[32,4,2048]{2,1,0:T(4,128)(2,1)S(1)} async-done(((bf16[32,4,2048]{2,1,0:T(4,128)(2,1)}), bf16[32,4,2048]{2,1,0:T(4,128)(2,1)S(1)}, u32[]{:S(2)}, u32[]{:S(2)}) %all-to-all-start.2) | async-done | bytes 524320 | tf_op jit(solution)/shard_map/all_to_all | solution.py:70
  279.2 0.1 all_to_all.22
  279.3 0.9 gather_fusion.1
  280.2 1.0 fusion.26
  (8 shorter events, 0.0 us)
Async XLA Ops:
  6.5 256.2 %copy-start = (bf16[32,2048]{1,0:T(8,128)(2,1)S(1)}, bf16[32,2048]{1,0:T(8,128)(2,1)}, u32[]{:S(2)}) copy-start(bf16[32,2048]{1,0:T(8,128)(2,1)} %param.9) | copy-start | bytes 393220
  6.5 205.5 %reduce-scatter.3.cloned.1.call-start = ((), (), s32[]{:S(2)}) async-start(), calls=%async_computation.5 | async-start | bytes 5242880 | tf_op jit(solution)/shard_map/reduce_scatter | solution.py:16
  156.1 106.6 %copy-start.1 = (bf16[128,2048]{1,0:T(8,128)(2,1)S(1)}, bf16[128,2048]{1,0:T(8,128)(2,1)}, u32[]{:S(2)}) copy-start(bf16[128,2048]{1,0:T(8,128)(2,1)} %param.6) | copy-start | bytes 1572868
  156.1 106.6 %copy-start.2 = (s32[128]{0:T(128)S(1)}, s32[128]{0:T(128)}, u32[]{:S(2)}) copy-start(s32[128]{0:T(128)} %param.7) | copy-start | bytes 1540
  156.1 99.1 %reduce-scatter.5.cloned.1.call-start = ((), (), s32[]{:S(2)}) async-start(), calls=%async_computation.6 | async-start | bytes 1572864 | tf_op jit(solution)/shard_map/reduce_scatter | solution.py:16
  257.3 21.9 %all-to-all-start.2 = ((bf16[32,4,2048]{2,1,0:T(4,128)(2,1)}), bf16[32,4,2048]{2,1,0:T(4,128)(2,1)S(1)}, u32[]{:S(2)}, u32[]{:S(2)}) async-start(bf16[32,4,2048]{2,1,0:T(4,128)(2,1)} %all_to_all.20), calls=%async_computation.4 | async-start | bytes 1048576 | tf_op jit(solution)/shard_map/all_to_all | solution.py:70
Sparse Core Ops, SparseCore 0:
  156.3 55.7 reduce-scatter.2
  214.5 40.6 reduce-scatter.4
